TPU v7x, 32 devices: a whole 2x2x4 slice. The times are simulated.
32 devices in a mesh: shard: 4 (over z), rep: 8 (over y, x, core).
Axes of the slice: x: 2, y: 2, z: 4, core: 2. Of those that a mesh axis runs over, the one named last changes fastest.
Arguments:
- inputs: bfloat16 [16, 1024, 1088], P('rep', 'shard'), may hold values from -6 to 6
- segments: int32 [16, 1024], P('rep'), may hold values from 0 to 2, never falling along the last dimension, each value on 1 to 640 neighbouring positions
- cotangent: bfloat16 [16, 1024, 1088], P('rep', 'shard'), may hold values from -6 to 6
- ln_gain: bfloat16 [2, 1088], P(None, 'shard'), may hold values from 0.099609375 to 1.8984375
- ln_bias: bfloat16 [2, 1088], P(None, 'shard'), may hold values from -3 to 3
- w_qkv: bfloat16 [1088, 3264], P(None, 'shard'), may hold values from -0.1875 to 0.1875
- qv_bias: bfloat16 [1, 2176], P(None, 'shard'), may hold values from -0.29882812 to 0.29882812
- w_out: bfloat16 [1088, 1088], P(None, 'shard'), may hold values from -3 to 3
- out_bias: bfloat16 [2, 1088], P(None, 'shard'), may hold values from -2 to 2
- w_fc1: bfloat16 [1088, 4352], P(None, 'shard'), may hold values from -0.1875 to 0.1875
- fc1_bias: bfloat16 [1, 4352], P(None, 'shard'), may hold values from -3 to 3
- w_fc2: bfloat16 [4352, 1088], P(None, 'shard'), may hold values from -0.09375 to 0.09375
Outputs:
- output: bfloat16 [16, 1024, 1088], P('rep', 'shard')
- d_inputs: bfloat16 [16, 1024, 1088], P('rep', 'shard')
- g_ln_gain: float32 [2, 1088], P(None, 'shard')
- g_ln_bias: float32 [2, 1088], P(None, 'shard')
- g_w_qkv: float32 [1088, 3264], P(None, 'shard')
- g_qv_bias: float32 [1, 2176], P(None, 'shard')
- g_w_out: float32 [1088, 1088], P(None, 'shard')
- g_out_bias: float32 [2, 1088], P(None, 'shard')
- g_w_fc1: float32 [1088, 4352], P(None, 'shard')
- g_fc1_bias: float32 [1, 4352], P(None, 'shard')
- g_w_fc2: float32 [4352, 1088], P(None, 'shard')
Inputs may be any that keep to these rules, and one draw needn't show every extreme that they name: `segments`: within a sequence the document numbers never fall; each of the three documents holds 1 to 640 tokens, and one holds exactly 640.
All inputs are finite; a program needn't handle non-finite values.
Results may differ from a plain program's by a relative error of at most 0.018.
Values may be sent and summed in bfloat16 or wider, within the bound.
A program may use at most 320 MiB of HBM per device.

v0:
```python
import jax
import jax.numpy as jnp
from jax import lax
from jax.sharding import PartitionSpec as P

HEADS = 17
HEAD_DIM = 64


def layer_norm(values, gain, bias):
    centered = values - jnp.mean(values, -1, keepdims=True)
    factor = lax.rsqrt(jnp.mean(centered * centered, -1, keepdims=True) + 1e-05)
    unit = centered * factor
    return (unit * gain + bias, unit, factor)


def norm_back(d_normed, unit, factor, gain):
    scaled = d_normed * gain
    return factor * (
        scaled
        - jnp.mean(scaled, -1, keepdims=True)
        - unit * jnp.mean(scaled * unit, -1, keepdims=True)
    )


def gelu_tanh(values):
    return jax.nn.gelu(values, approximate=True)


def block_scores(queries, key_block, query_pos, query_seg, pos_block, seg_block):
    raw_scores = jnp.einsum(
        "qhe,khe->hqk", queries, key_block, preferred_element_type=jnp.float32
    ) * HEAD_DIM ** (-0.5)
    allowed = (pos_block[None, :] <= query_pos[:, None]) & (
        seg_block[None, :] == query_seg[:, None]
    )
    return (raw_scores, allowed[None])


def split_blocks(key_all, value_all, seg_row):
    total_rows = key_all.shape[0]
    block_rows = min(512, total_rows)
    block_count = total_rows // block_rows
    key_blocks = key_all.reshape(block_count, block_rows, HEADS, HEAD_DIM)
    value_blocks = value_all.reshape(block_count, block_rows, HEADS, HEAD_DIM)
    pos_blocks = jnp.arange(total_rows, dtype=jnp.int32).reshape(block_count, block_rows)
    seg_blocks = seg_row.reshape(block_count, block_rows)
    return (key_blocks, value_blocks, pos_blocks, seg_blocks)


def attention_forward(queries, key_all, value_all, query_pos, query_seg, seg_row):
    key_blocks, value_blocks, pos_blocks, seg_blocks = split_blocks(key_all, value_all, seg_row)
    row_count = queries.shape[0]

    def gather_stats(state_pair, block_item):
        run_max, run_sum = state_pair
        key_block, pos_block, seg_block = block_item
        raw_scores, allowed = block_scores(
            queries, key_block, query_pos, query_seg, pos_block, seg_block
        )
        masked = jnp.where(allowed, raw_scores, -1e30)
        new_max = jnp.maximum(run_max, jnp.max(masked, -1))
        expo = jnp.where(allowed, jnp.exp(masked - new_max[..., None]), 0.0)
        run_sum = run_sum * jnp.exp(run_max - new_max) + jnp.sum(expo, -1)
        return ((new_max, run_sum), None)

    start_max = jnp.full((HEADS, row_count), -1e30, jnp.float32)
    start_sum = jnp.zeros((HEADS, row_count), jnp.float32)
    (run_max, run_sum), _ = lax.scan(
        gather_stats, (start_max, start_sum), (key_blocks, pos_blocks, seg_blocks)
    )
    log_total = run_max + jnp.log(run_sum)

    def gather_values(accum_out, block_item):
        key_block, value_block, pos_block, seg_block = block_item
        raw_scores, allowed = block_scores(
            queries, key_block, query_pos, query_seg, pos_block, seg_block
        )
        attn_probs = jnp.where(allowed, jnp.exp(raw_scores - log_total[..., None]), 0.0).astype(
            jnp.bfloat16
        )
        return (
            accum_out
            + jnp.einsum(
                "hqk,khe->qhe", attn_probs, value_block, preferred_element_type=jnp.float32
            ),
            None,
        )

    start_out = jnp.zeros((row_count, HEADS, HEAD_DIM), jnp.float32)
    accum_out, _ = lax.scan(
        gather_values, start_out, (key_blocks, value_blocks, pos_blocks, seg_blocks)
    )
    return (accum_out, log_total)


def attention_backward(
    queries, key_all, value_all, d_mixed, log_total, query_pos, query_seg, seg_row
):
    key_blocks, value_blocks, pos_blocks, seg_blocks = split_blocks(key_all, value_all, seg_row)
    row_count = queries.shape[0]
    scale = HEAD_DIM ** (-0.5)

    def probs_and_grads(block_item):
        key_block, value_block, pos_block, seg_block = block_item
        raw_scores, allowed = block_scores(
            queries, key_block, query_pos, query_seg, pos_block, seg_block
        )
        attn_probs = jnp.where(allowed, jnp.exp(raw_scores - log_total[..., None]), 0.0)
        d_probs = jnp.einsum(
            "qhe,khe->hqk", d_mixed, value_block, preferred_element_type=jnp.float32
        )
        return (attn_probs, d_probs)

    def gather_delta(row_delta, block_item):
        attn_probs, d_probs = probs_and_grads(block_item)
        return (row_delta + jnp.sum(attn_probs * d_probs, -1), None)

    blocks_all = (key_blocks, value_blocks, pos_blocks, seg_blocks)
    row_delta, _ = lax.scan(gather_delta, jnp.zeros((HEADS, row_count), jnp.float32), blocks_all)

    def gather_grads(d_queries, block_item):
        key_block = block_item[0]
        attn_probs, d_probs = probs_and_grads(block_item)
        d_scores = (attn_probs * (d_probs - row_delta[..., None])).astype(jnp.bfloat16)
        d_queries = (
            d_queries
            + jnp.einsum("hqk,khe->qhe", d_scores, key_block, preferred_element_type=jnp.float32)
            * scale
        )
        key_grad = (
            jnp.einsum("hqk,qhe->khe", d_scores, queries, preferred_element_type=jnp.float32)
            * scale
        )
        value_grad = jnp.einsum(
            "hqk,qhe->khe",
            attn_probs.astype(jnp.bfloat16),
            d_mixed,
            preferred_element_type=jnp.float32,
        )
        block_rows = key_block.shape[0]
        term = jnp.concatenate(
            [key_grad.reshape(block_rows, -1), value_grad.reshape(block_rows, -1)], 1
        )
        return (d_queries, term)

    start_grad = jnp.zeros((row_count, HEADS, HEAD_DIM), jnp.float32)
    d_queries, terms = lax.scan(gather_grads, start_grad, blocks_all)
    return (d_queries, terms.reshape(key_all.shape[0], -1))


def shards(
    inputs,
    segments,
    cotangent,
    ln_gain,
    ln_bias,
    w_qkv,
    qv_bias,
    w_out,
    out_bias,
    w_fc1,
    fc1_bias,
    w_fc2,
):
    row_count = inputs.shape[1]
    features = inputs.shape[2]
    shard_index = lax.axis_index("shard")
    query_pos = shard_index * row_count + jnp.arange(row_count, dtype=jnp.int32)
    gathered = (
        lax.all_gather(ln_gain, "shard", axis=1, tiled=True),
        lax.all_gather(ln_bias, "shard", axis=1, tiled=True),
        lax.all_gather(w_qkv, "shard", axis=1, tiled=True),
        lax.all_gather(qv_bias, "shard", axis=1, tiled=True),
        lax.all_gather(w_out, "shard", axis=1, tiled=True),
        lax.all_gather(out_bias, "shard", axis=1, tiled=True),
        lax.all_gather(w_fc1, "shard", axis=1, tiled=True),
        lax.all_gather(fc1_bias, "shard", axis=1, tiled=True),
        lax.all_gather(w_fc2, "shard", axis=1, tiled=True),
    )
    gain_rows = gathered[0].astype(jnp.float32)
    bias_rows = gathered[1].astype(jnp.float32)
    qv_row = gathered[3].astype(jnp.float32)
    out_rows = gathered[5].astype(jnp.float32)
    fc1_row = gathered[7].astype(jnp.float32)
    bias_full = jnp.concatenate(
        [qv_row[0, :features], jnp.zeros((features,), jnp.float32), qv_row[0, features:]]
    )

    def forward_step(marker, item):
        token_bf, seg_row = item
        tokens = token_bf.astype(jnp.float32)
        query_seg = lax.dynamic_slice_in_dim(seg_row, shard_index * row_count, row_count)
        normed_f32, unit_one, factor_one = layer_norm(tokens, gain_rows[0], bias_rows[0])
        normed_one = normed_f32.astype(jnp.bfloat16)
        qkv = (
            jnp.dot(normed_one, gathered[2], preferred_element_type=jnp.float32) + bias_full
        ).astype(jnp.bfloat16)
        queries = qkv[:, :features].reshape(row_count, HEADS, HEAD_DIM)
        key_local = qkv[:, features : 2 * features]
        value_local = qkv[:, 2 * features :]
        key_all, value_all = (
            lax.all_gather(key_local, "shard", axis=0, tiled=True),
            lax.all_gather(value_local, "shard", axis=0, tiled=True),
        )
        attn_out, log_total = attention_forward(
            queries, key_all, value_all, query_pos, query_seg, seg_row
        )
        attn_mixed = attn_out.reshape(row_count, features).astype(jnp.bfloat16)
        branch = jnp.dot(attn_mixed, gathered[4], preferred_element_type=jnp.float32) + out_rows[0]
        residual = tokens + branch
        normed_f32, unit_two, factor_two = layer_norm(residual, gain_rows[1], bias_rows[1])
        normed_two = normed_f32.astype(jnp.bfloat16)
        pre_act = jnp.dot(normed_two, gathered[6], preferred_element_type=jnp.float32) + fc1_row[0]
        activated = gelu_tanh(pre_act).astype(jnp.bfloat16)
        output = residual + (
            jnp.dot(activated, gathered[8], preferred_element_type=jnp.float32) + out_rows[1]
        )
        saved = (
            normed_one,
            unit_one,
            factor_one,
            queries,
            key_local,
            value_local,
            log_total,
            attn_mixed,
            unit_two,
            factor_two,
            normed_two,
            pre_act,
        )
        return (marker, (output.astype(jnp.bfloat16), saved, ()))

    _, (outputs, saved_all, kept_all) = lax.scan(
        forward_step, jnp.zeros((), jnp.float32), (inputs, segments)
    )
    regathered = (
        lax.all_gather(ln_gain, "shard", axis=1, tiled=True),
        lax.all_gather(ln_bias, "shard", axis=1, tiled=True),
        lax.all_gather(w_qkv, "shard", axis=1, tiled=True),
        lax.all_gather(qv_bias, "shard", axis=1, tiled=True),
        lax.all_gather(w_out, "shard", axis=1, tiled=True),
        lax.all_gather(out_bias, "shard", axis=1, tiled=True),
        lax.all_gather(w_fc1, "shard", axis=1, tiled=True),
        lax.all_gather(fc1_bias, "shard", axis=1, tiled=True),
        lax.all_gather(w_fc2, "shard", axis=1, tiled=True),
    )

    def pair_source(key_local, value_local):
        return (
            lax.all_gather(key_local, "shard", axis=0, tiled=True),
            lax.all_gather(value_local, "shard", axis=0, tiled=True),
        )

    back_gains = regathered[0].astype(jnp.float32)

    def backward_step(sums, item):
        saved, kept_pair, d_output, seg_row = item
        (
            normed_one,
            unit_one,
            factor_one,
            queries,
            key_local,
            value_local,
            log_total,
            attn_mixed,
            unit_two,
            factor_two,
            normed_two,
            pre_act,
        ) = saved
        query_seg = lax.dynamic_slice_in_dim(seg_row, shard_index * row_count, row_count)
        key_back, value_back = pair_source(key_local, value_local)
        activated_f32, gelu_pull = jax.vjp(gelu_tanh, pre_act)
        activated = activated_f32.astype(jnp.bfloat16)
        d_out_f32 = d_output.astype(jnp.float32)
        g_fc2 = jnp.einsum("tf,td->fd", activated, d_output, preferred_element_type=jnp.float32)
        d_act = jnp.einsum("td,fd->tf", d_output, regathered[8], preferred_element_type=jnp.float32)
        d_pre = gelu_pull(d_act)[0].astype(jnp.bfloat16)
        g_fc1 = jnp.einsum("td,tf->df", normed_two, d_pre, preferred_element_type=jnp.float32)
        g_fc1_row = jnp.sum(d_pre.astype(jnp.float32), 0)
        d_norm_two = jnp.einsum(
            "tf,df->td", d_pre, regathered[6], preferred_element_type=jnp.float32
        )
        d_residual = d_out_f32 + norm_back(d_norm_two, unit_two, factor_two, back_gains[1])
        g_gain_two = jnp.sum(d_norm_two * unit_two, 0)
        g_bias_two = jnp.sum(d_norm_two, 0)
        d_branch = d_residual.astype(jnp.bfloat16)
        g_wout = jnp.einsum("td,te->de", attn_mixed, d_branch, preferred_element_type=jnp.float32)
        g_out_zero = jnp.sum(d_branch.astype(jnp.float32), 0)
        g_out_one = jnp.sum(d_out_f32, 0)
        d_mixed = jnp.einsum(
            "te,de->td", d_branch, regathered[4], preferred_element_type=jnp.float32
        )
        d_mixed = d_mixed.astype(jnp.bfloat16).reshape(row_count, HEADS, HEAD_DIM)
        d_queries, kv_term = attention_backward(
            queries, key_back, value_back, d_mixed, log_total, query_pos, query_seg, seg_row
        )
        kv_grad = lax.psum_scatter(
            kv_term.astype(jnp.bfloat16), "shard", scatter_dimension=0, tiled=True
        ).astype(jnp.float32)
        d_qkv = jnp.concatenate([d_queries.reshape(row_count, features), kv_grad], 1).astype(
            jnp.bfloat16
        )
        g_wqkv = jnp.einsum("td,tc->dc", normed_one, d_qkv, preferred_element_type=jnp.float32)
        d_qkv_f32 = d_qkv.astype(jnp.float32)
        g_qv_row = jnp.concatenate(
            [jnp.sum(d_qkv_f32[:, :features], 0), jnp.sum(d_qkv_f32[:, 2 * features :], 0)]
        )
        d_norm_one = jnp.einsum(
            "tc,dc->td", d_qkv, regathered[2], preferred_element_type=jnp.float32
        )
        d_tokens = d_residual + norm_back(d_norm_one, unit_one, factor_one, back_gains[0])
        g_gain_one = jnp.sum(d_norm_one * unit_one, 0)
        g_bias_one = jnp.sum(d_norm_one, 0)
        local_grads = (
            jnp.stack([g_gain_one, g_gain_two]),
            jnp.stack([g_bias_one, g_bias_two]),
            g_wqkv,
            g_qv_row[None],
            g_wout,
            jnp.stack([g_out_zero, g_out_one]),
            g_fc1,
            g_fc1_row[None],
            g_fc2,
        )
        new_sums = tuple((old + new for old, new in zip(sums, local_grads)))
        return (new_sums, d_tokens.astype(jnp.bfloat16))

    zero_sums = tuple((jnp.zeros(item.shape, jnp.float32) for item in regathered))
    grad_sums, d_inputs = lax.scan(
        backward_step, zero_sums, (saved_all, kept_all, cotangent, segments)
    )
    owned = (
        lax.psum_scatter(
            grad_sums[0].astype(jnp.bfloat16), "shard", scatter_dimension=1, tiled=True
        ).astype(jnp.float32),
        lax.psum_scatter(
            grad_sums[1].astype(jnp.bfloat16), "shard", scatter_dimension=1, tiled=True
        ).astype(jnp.float32),
        lax.psum_scatter(
            grad_sums[2].astype(jnp.bfloat16), "shard", scatter_dimension=1, tiled=True
        ).astype(jnp.float32),
        lax.psum_scatter(
            grad_sums[3].astype(jnp.bfloat16), "shard", scatter_dimension=1, tiled=True
        ).astype(jnp.float32),
        lax.psum_scatter(
            grad_sums[4].astype(jnp.bfloat16), "shard", scatter_dimension=1, tiled=True
        ).astype(jnp.float32),
        lax.psum_scatter(
            grad_sums[5].astype(jnp.bfloat16), "shard", scatter_dimension=1, tiled=True
        ).astype(jnp.float32),
        lax.psum_scatter(
            grad_sums[6].astype(jnp.bfloat16), "shard", scatter_dimension=1, tiled=True
        ).astype(jnp.float32),
        lax.psum_scatter(
            grad_sums[7].astype(jnp.bfloat16), "shard", scatter_dimension=1, tiled=True
        ).astype(jnp.float32),
        lax.psum_scatter(
            grad_sums[8].astype(jnp.bfloat16), "shard", scatter_dimension=1, tiled=True
        ).astype(jnp.float32),
    )
    summed = (
        lax.psum(owned[0].astype(jnp.bfloat16), "rep").astype(jnp.float32),
        lax.psum(owned[1].astype(jnp.bfloat16), "rep").astype(jnp.float32),
        lax.psum(owned[2].astype(jnp.bfloat16), "rep").astype(jnp.float32),
        lax.psum(owned[3].astype(jnp.bfloat16), "rep").astype(jnp.float32),
        lax.psum(owned[4].astype(jnp.bfloat16), "rep").astype(jnp.float32),
        lax.psum(owned[5].astype(jnp.bfloat16), "rep").astype(jnp.float32),
        lax.psum(owned[6].astype(jnp.bfloat16), "rep").astype(jnp.float32),
        lax.psum(owned[7].astype(jnp.bfloat16), "rep").astype(jnp.float32),
        lax.psum(owned[8].astype(jnp.bfloat16), "rep").astype(jnp.float32),
    )
    return (outputs, d_inputs) + tuple(summed)


def solution(mesh):
    placed = (
        P("rep", "shard", None),
        P("rep", None),
        P("rep", "shard", None),
        P(None, "shard"),
        P(None, "shard"),
        P(None, "shard"),
        P(None, "shard"),
        P(None, "shard"),
        P(None, "shard"),
        P(None, "shard"),
        P(None, "shard"),
        P(None, "shard"),
    )
    return jax.shard_map(
        shards,
        mesh=mesh,
        in_specs=placed,
        out_specs=(
            P("rep", "shard", None),
            P("rep", "shard", None),
            P(None, "shard"),
            P(None, "shard"),
            P(None, "shard"),
            P(None, "shard"),
            P(None, "shard"),
            P(None, "shard"),
            P(None, "shard"),
            P(None, "shard"),
            P(None, "shard"),
        ),
        check_vma=False,
    )
```

profile of v0, /device:TPU:0, one launch (start us, length us, event | category | flops | bytes accessed | tf_op | source)
XLA Modules:
  0.0 2230.3 jit_solution(1445620045260461774)
XLA Ops:
  78.5 122.9 %all-gather.20.cloned.1.call-done = bf16[1088,3264]{0,1:T(8,128)(2,1)} async-done(((bf16[1088,816]{0,1:T(8,128)(2,1)}), bf16[1088,3264]{0,1:T(8,128)(2,1)}) %all-gather.20.cloned.1.call-update) | async-done | bytes 7102480 | tf_op jit(solution)/shard_map/all_gather | solution.py:173
  213.1 155.4 %all-gather.26.cloned.1.call-done = bf16[4352,1088]{0,1:T(8,128)(2,1)} async-done(((bf16[4352,272]{0,1:T(8,128)(2,1)}), bf16[4352,1088]{0,1:T(8,128)(2,1)}) %all-gather.26.cloned.1.call-update) | async-done | bytes 9469968 | tf_op jit(solution)/shard_map/all_gather | solution.py:179
  382.6 162.5 %all-gather.24.cloned.1.call-done = bf16[1088,4352]{0,1:T(8,128)(2,1)} async-done(((bf16[1088,1088]{0,1:T(8,128)(2,1)}), bf16[1088,4352]{0,1:T(8,128)(2,1)}) %all-gather.24.cloned.1.call-update) | async-done | bytes 9469968 | tf_op jit(solution)/shard_map/all_gather | solution.py:177
  565.6 321.6 %while.180 = (s32[]{:T(128)}, bf16[2,256,1088]{1,2,0:T(8,128)(2,1)}, bf16[2,256,1088]{1,2,0:T(8,128)(2,1)}, f32[2,256,1088]{1,2,0:T(8,128)}, f32[2,256,1]{1,2,0:...) while((s32[]{:T(128)}, bf16[2,256,1088]{1,2,0:T(8,128)(2,1)}, ...), condition=%wide.region_11.12_spmd.clone, body=%wide.region_0.11_spmd.clone.sunk | while | flops 8181739520 | bytes 234688240 | solution.py:235
  578.8 43.6 %all-gather.28.cloned.1.call-done = bf16[1024,1088]{0,1:T(8,128)(2,1)} async-done(((bf16[256,1088]{0,1:T(8,128)(2,1)}), bf16[1024,1088]{0,1:T(8,128)(2,1)}) %all-gather.28.cloned.1.call-update) | async-done | bytes 2228240 | tf_op jit(solution)/shard_map/while/body/eval_jaxpr/all_gather | solution.py:204
  629.6 40.8 %all-gather.30.cloned.1.call-done = bf16[1024,1088]{0,1:T(8,128)(2,1)} async-done(((bf16[256,1088]{0,1:T(8,128)(2,1)}), bf16[1024,1088]{0,1:T(8,128)(2,1)}) %all-gather.30.cloned.1.call-update) | async-done | bytes 2228240 | tf_op jit(solution)/shard_map/while/body/eval_jaxpr/all_gather | solution.py:203
  739.4 43.5 %all-gather.28.cloned.1.call-done = bf16[1024,1088]{0,1:T(8,128)(2,1)} async-done(((bf16[256,1088]{0,1:T(8,128)(2,1)}), bf16[1024,1088]{0,1:T(8,128)(2,1)}) %all-gather.28.cloned.1.call-update) | async-done | bytes 2228240 | tf_op jit(solution)/shard_map/while/body/eval_jaxpr/all_gather | solution.py:204
  790.1 41.0 %all-gather.30.cloned.1.call-done = bf16[1024,1088]{0,1:T(8,128)(2,1)} async-done(((bf16[256,1088]{0,1:T(8,128)(2,1)}), bf16[1024,1088]{0,1:T(8,128)(2,1)}) %all-gather.30.cloned.1.call-update) | async-done | bytes 2228240 | tf_op jit(solution)/shard_map/while/body/eval_jaxpr/all_gather | solution.py:203
  888.3 543.1 %while.183 = (s32[]{:T(128)}, f32[2,1088]{1,0:T(2,128)}, f32[2,1088]{1,0:T(2,128)}, f32[1088,3264]{1,0:T(8,128)}, f32[1,2176]{1,0:T(1,128)}, /*index=5*/f32[1088...) while((s32[]{:T(128)}, f32[2,1088]{1,0:T(2,128)}, ...), condition=%wide.region_32.33_spmd.clone, body=%wide.region_12.32_spmd.clone.sunk | while | flops 16666535936 | bytes 520477184 | solution.py:333
  966.4 40.8 %all-gather.32.cloned.1.call-done = bf16[1,1024,1088]{1,2,0:T(8,128)(2,1)} async-done(((bf16[1,256,1088]{1,2,0:T(8,128)(2,1)}), bf16[1,1024,1088]{1,2,0:T(8,128)(2,1)}) %all-gather.32.cloned.1.call-update) | async-done | bytes 2228240 | tf_op jit(solution)/shard_map/while/body/eval_jaxpr/all_gather | solution.py:252
  1028.4 40.5 %while.187 = (s32[]{:T(128)}, f32[256,17,64]{0,2,1:T(8,128)}, bf16[2,512,2176]{2,1,0:T(8,128)(2,1)}, bf16[2,512,17,64]{1,3,2,0:T(8,128)(2,1)}, s32[2,512]{1,0:T(...) while((s32[]{:T(128)}, f32[256,17,64]{0,2,1:T(8,128)}, ...), condition=%wide.region_19.19_spmd.clone, body=%wide.region_18.18_spmd.clone.sunk | while | flops 1455144960 | bytes 63964336 | solution.py:148
  1095.2 53.1 %reduce-scatter.43.cloned.1.call-done = bf16[256,2176]{1,0:T(8,128)(2,1)} async-done(((bf16[1024,2176]{1,0:T(8,128)(2,1)}), bf16[256,2176]{1,0:T(8,128)(2,1)}) %reduce-scatter.43.cloned.1.call-update) | async-done | bytes 1114128 | tf_op jit(solution)/shard_map/while/body/eval_jaxpr/reduce_scatter | solution.py:301
  1196.7 21.8 all-gather.34.cloned.1.call-done
  1225.7 41.0 %all-gather.32.cloned.1.call-done = bf16[1,1024,1088]{1,2,0:T(8,128)(2,1)} async-done(((bf16[1,256,1088]{1,2,0:T(8,128)(2,1)}), bf16[1,1024,1088]{1,2,0:T(8,128)(2,1)}) %all-gather.32.cloned.1.call-update) | async-done | bytes 2228240 | tf_op jit(solution)/shard_map/while/body/eval_jaxpr/all_gather | solution.py:252
  1287.8 40.5 %while.187 = (s32[]{:T(128)}, f32[256,17,64]{0,2,1:T(8,128)}, bf16[2,512,2176]{2,1,0:T(8,128)(2,1)}, bf16[2,512,17,64]{1,3,2,0:T(8,128)(2,1)}, s32[2,512]{1,0:T(...) while((s32[]{:T(128)}, f32[256,17,64]{0,2,1:T(8,128)}, ...), condition=%wide.region_19.19_spmd.clone, body=%wide.region_18.18_spmd.clone.sunk | while | flops 1455144960 | bytes 63964336 | solution.py:148
  1364.1 43.7 %reduce-scatter.43.cloned.1.call-done = bf16[256,2176]{1,0:T(8,128)(2,1)} async-done(((bf16[1024,2176]{1,0:T(8,128)(2,1)}), bf16[256,2176]{1,0:T(8,128)(2,1)}) %reduce-scatter.43.cloned.1.call-update) | async-done | bytes 1114128 | tf_op jit(solution)/shard_map/while/body/eval_jaxpr/reduce_scatter | solution.py:301
  1500.5 82.4 %reduce-scatter.33.cloned.1.call-done = bf16[816,1088]{1,0:T(8,128)(2,1)} async-done(((bf16[3264,1088]{1,0:T(8,128)(2,1)}), bf16[816,1088]{1,0:T(8,128)(2,1)}) %reduce-scatter.33.cloned.1.call-update) | async-done | bytes 1775632
  1586.8 169.4 %reduce-scatter.39.cloned.1.call-done = bf16[1088,1088]{1,0:T(8,128)(2,1)} async-done(((bf16[4352,1088]{1,0:T(8,128)(2,1)}), bf16[1088,1088]{1,0:T(8,128)(2,1)}) %reduce-scatter.39.cloned.1.call-update) | async-done | bytes 2367504
  1761.4 49.3 %reduce-scatter.25.cloned.1.call-done = bf16[1088,272]{0,1:T(8,128)(2,1)} async-done(((bf16[1088,1088]{0,1:T(8,128)(2,1)}), bf16[1088,272]{0,1:T(8,128)(2,1)}) %reduce-scatter.25.cloned.1.call-update) | async-done | bytes 591888 | tf_op jit(solution)/shard_map/reduce_scatter | solution.py:349
  1810.7 163.8 %reduce-scatter.27.cloned.1.call-done = bf16[4352,272]{0,1:T(8,128)(2,1)} async-done(((bf16[4352,1088]{0,1:T(8,128)(2,1)}), bf16[4352,272]{0,1:T(8,128)(2,1)}) %reduce-scatter.27.cloned.1.call-update) | async-done | bytes 2367504 | tf_op jit(solution)/shard_map/reduce_scatter | solution.py:361
  1974.5 23.5 %reduce-scatter.37.cloned.1.call-done = bf16[272,2]{1,0:T(8,128)(2,1)} async-done(((bf16[1088,2]{1,0:T(8,128)(2,1)}), bf16[272,2]{1,0:T(8,128)(2,1)}) %reduce-scatter.37.cloned.1.call-update) | async-done | bytes 1104
  2062.9 28.5 %reduce-scatter.41.cloned.1.call-done = bf16[1088,1]{1,0:T(8,128)(2,1)} async-done(((bf16[4352,1]{1,0:T(8,128)(2,1)}), bf16[1088,1]{1,0:T(8,128)(2,1)}) %reduce-scatter.41.cloned.1.call-update) | async-done | bytes 2192
  2092.5 25.0 %all-reduce.2 = (bf16[2,272]{1,0:T(2,128)(2,1)S(1)}, bf16[2,272]{1,0:T(2,128)(2,1)S(1)}, bf16[1,544]{1,0:T(2,128)(2,1)S(1)}, bf16[2,272]{1,0:T(2,128)(2,1)S(1)}, bf16[1,1088]{1,0:T(2,128)(2,1)S(1)}) all-reduce(bf16[2,272]{1,0:T(2,128)(2,1)S(1)} %copy.214, bf16[2,272]{1,0:T(2,128)(2,1)S(1)} %copy.216, ...), channel_id=1, replica_groups=mesh['shard'=4,'rep'=8] {'rep'}, use_global_device_ids=true, to_apply=%region_34.35 | all-reduce | flops 3264 | bytes 13056 | tf_op jit(solution)/shard_map/psum | solution.py:366
  2120.4 91.0 %all-reduce.7.cloned.1.call-done = (bf16[1088,816]{1,0:T(8,128)(2,1)}, bf16[1088,272]{0,1:T(8,128)(2,1)}, bf16[1088,1088]{1,0:T(8,128)(2,1)}, bf16[4352,272]{0,1:T(8,128)(2,1)}) async-done(((bf16[1088,816]{1,0:T(8,128)(2,1)}, bf16[1088,272]{0,1:T(8,128)(2,1)}, bf16[1088,1088]{1,0:T(8,128)(2,1)}, bf16[4352,272]{0,1:T(8,128)(2,1)}), (bf16[1088,816]{1,0:T(8,128)(2,1)}, bf16[1088,272]{0,1:T(8,128)(2,1)}, ...) | async-done | bytes 7102480 | tf_op jit(solution)/shard_map/psum | solution.py:368
  (671 shorter events, 806.6 us)
Async XLA Ops:
  7.2 66.0 %all-gather.22.cloned.1.call-start = ((), (), s32[]{:S(2)}) async-start(), calls=%async_computation.11 | async-start | bytes 3133440 | tf_op jit(solution)/shard_map/all_gather | solution.py:175
  7.9 193.5 %all-gather.20.cloned.1.call-start = ((), (), s32[]{:S(2)}) async-start(), calls=%async_computation.10 | async-start | bytes 9400320 | tf_op jit(solution)/shard_map/all_gather | solution.py:173
  8.7 359.8 %all-gather.26.cloned.1.call-start = ((), (), s32[]{:S(2)}) async-start(), calls=%async_computation.13 | async-start | bytes 11837440 | tf_op jit(solution)/shard_map/all_gather | solution.py:179
  9.4 535.7 %all-gather.24.cloned.1.call-start = ((), (), s32[]{:S(2)}) async-start(), calls=%async_computation.12 | async-start | bytes 12533760 | tf_op jit(solution)/shard_map/all_gather | solution.py:177
  566.0 56.4 %all-gather.28.cloned.1.call-start = ((), (), s32[]{:S(2)}) async-start(), calls=%async_computation.24 | async-start | bytes 2785280 | tf_op jit(solution)/shard_map/while/body/eval_jaxpr/all_gather | solution.py:204
  575.6 94.8 %all-gather.30.cloned.1.call-start = ((), (), s32[]{:S(2)}) async-start(), calls=%async_computation.25 | async-start | bytes 2785280 | tf_op jit(solution)/shard_map/while/body/eval_jaxpr/all_gather | solution.py:203
  726.5 56.4 %all-gather.28.cloned.1.call-start = ((), (), s32[]{:S(2)}) async-start(), calls=%async_computation.24 | async-start | bytes 2785280 | tf_op jit(solution)/shard_map/while/body/eval_jaxpr/all_gather | solution.py:204
  736.1 94.9 %all-gather.30.cloned.1.call-start = ((), (), s32[]{:S(2)}) async-start(), calls=%async_computation.25 | async-start | bytes 2785280 | tf_op jit(solution)/shard_map/while/body/eval_jaxpr/all_gather | solution.py:203
  910.2 49.0 %all-gather.34.cloned.1.call-start = ((), (), s32[]{:S(2)}) async-start(), calls=%async_computation.27 | async-start | bytes 2785280 | tf_op jit(solution)/shard_map/while/body/eval_jaxpr/all_gather | solution.py:253
  912.2 94.9 %all-gather.32.cloned.1.call-start = ((), (), s32[]{:S(2)}) async-start(), calls=%async_computation.26 | async-start | bytes 2785280 | tf_op jit(solution)/shard_map/while/body/eval_jaxpr/all_gather | solution.py:252
  914.2 234.1 %reduce-scatter.43.cloned.1.call-start = ((), (), s32[]{:S(2)}) async-start(), calls=%async_computation.28 | async-start | bytes 5570560 | tf_op jit(solution)/shard_map/while/body/eval_jaxpr/reduce_scatter | solution.py:301
  1167.4 51.1 %all-gather.34.cloned.1.call-start = ((), (), s32[]{:S(2)}) async-start(), calls=%async_computation.27 | async-start | bytes 2785280 | tf_op jit(solution)/shard_map/while/body/eval_jaxpr/all_gather | solution.py:253
  1169.4 97.2 %all-gather.32.cloned.1.call-start = ((), (), s32[]{:S(2)}) async-start(), calls=%async_computation.26 | async-start | bytes 2785280 | tf_op jit(solution)/shard_map/while/body/eval_jaxpr/all_gather | solution.py:252
  1171.4 236.4 %reduce-scatter.43.cloned.1.call-start = ((), (), s32[]{:S(2)}) async-start(), calls=%async_computation.28 | async-start | bytes 5570560 | tf_op jit(solution)/shard_map/while/body/eval_jaxpr/reduce_scatter | solution.py:301
  1431.4 151.5 %reduce-scatter.33.cloned.1.call-start = ((), (), s32[]{:S(2)}) async-start(), calls=%async_computation.18 | async-start | bytes 9400320
  1451.4 304.9 %reduce-scatter.39.cloned.1.call-start = ((), (), s32[]{:S(2)}) async-start(), calls=%async_computation.21 | async-start | bytes 12533760
  1477.0 333.7 %reduce-scatter.25.cloned.1.call-start = ((), (), s32[]{:S(2)}) async-start(), calls=%async_computation.14 | async-start | bytes 3133440 | tf_op jit(solution)/shard_map/reduce_scatter | solution.py:349
  1482.8 491.7 %reduce-scatter.27.cloned.1.call-start = ((), (), s32[]{:S(2)}) async-start(), calls=%async_computation.15 | async-start | bytes 11837440 | tf_op jit(solution)/shard_map/reduce_scatter | solution.py:361
  1494.1 503.9 %reduce-scatter.37.cloned.1.call-start = ((), (), s32[]{:S(2)}) async-start(), calls=%async_computation.20 | async-start | bytes 348160
  1495.7 522.9 %reduce-scatter.31.cloned.1.call-start = ((), (), s32[]{:S(2)}) async-start(), calls=%async_computation.17 | async-start | bytes 348160
  1496.7 542.6 %reduce-scatter.29.cloned.1.call-start = ((), (), s32[]{:S(2)}) async-start(), calls=%async_computation.16 | async-start | bytes 348160
  1497.7 564.2 %reduce-scatter.35.cloned.1.call-start = ((), (), s32[]{:S(2)}) async-start(), calls=%async_computation.19 | async-start | bytes 696320
  1498.9 592.5 %reduce-scatter.41.cloned.1.call-start = ((), (), s32[]{:S(2)}) async-start(), calls=%async_computation.22 | async-start | bytes 1392640
  1500.4 711.0 %all-reduce.7.cloned.1.call-start = ((), (), s32[]{:S(2)}) async-start(), calls=%async_computation.23 | async-start | bytes 14901248 | tf_op jit(solution)/shard_map/psum | solution.py:368
  (132 other events, 815.5 us)
Sparse Core Ops, SparseCore 0:
  9.6 56.0 all-gather.21
  67.2 134.1 all-gather.19
  203.0 165.4 all-gather.25
  370.5 174.5 all-gather.23
  575.8 46.5 all-gather.27
  623.8 46.5 all-gather.29
  736.3 46.5 all-gather.27
  784.4 46.5 all-gather.29
  912.5 46.5 all-gather.33
  960.6 46.5 all-gather.31
  1069.0 79.2 reduce-scatter.42
  1169.6 48.8 all-gather.33
  1220.0 46.5 all-gather.31
  1328.5 79.2 reduce-scatter.42
  1451.5 131.3 reduce-scatter.32
  1585.1 171.1 reduce-scatter.38
  1759.0 51.6 reduce-scatter.24
  1812.9 161.5 reduce-scatter.26
  1976.7 21.1 reduce-scatter.36
  2000.1 18.4 reduce-scatter.30
  2020.8 18.4 reduce-scatter.28
  2041.6 20.2 reduce-scatter.34
  2064.7 26.6 reduce-scatter.40
  2095.5 115.8 all-reduce.6
where the time goes:
time: 2240 us; the launch traced here: 2230 us
  waiting for transfers between devices  1500 us (67%)
  matrix products  279 us (12%)
  local copies, waits for them, and re-layouts  248 us (11%)
  blocking collectives  81.7 us (4%)
  other arithmetic  72.3 us (3%)
  loops' own time  29.5 us (1%)
    unnamed x21, waiting for transfers between devices  367 us
    reduce_scatter x1, waiting for transfers between devices, shards(): lax.psum_scatter(grad_sums[8].astype(jnp.bfloat16), 'shard', scatter_dime...  164 us
    all_gather x1, waiting for transfers between devices, shards(): lax.all_gather(w_fc1, 'shard', axis=1, tiled=True)  162 us
    all_gather x1, waiting for transfers between devices, shards(): lax.all_gather(w_fc2, 'shard', axis=1, tiled=True)  155 us
    all_gather x1, waiting for transfers between devices, shards(): lax.all_gather(w_qkv, 'shard', axis=1, tiled=True)  123 us
    unnamed x57, local copies, waits for them, and re-layouts  99.6 us
    reduce_scatter x2, waiting for transfers between devices, backward_step(): lax.psum_scatter(kv_term.astype(jnp.bfloat16), 'shard', scatter_dimension...  96.9 us
    psum x1, waiting for transfers between devices, shards(): lax.psum(owned[2].astype(jnp.bfloat16), 'rep').astype(jnp.float32)  91 us
  transfers between devices with their start and end apart: 24, of which 23 were waited for; matrix products, arithmetic and copies ran while one was open for 11% of the time, Pallas kernels for 0%

commit v1 on v0

--- a/solution.py
+++ b/solution.py
@@ -1,6 +1,8 @@
 import jax
 import jax.numpy as jnp
 from jax import lax
+from jax.experimental import pallas as pl
+from jax.experimental.pallas import tpu as pltpu
 from jax.sharding import PartitionSpec as P
 
 HEADS = 17
@@ -376,7 +378,368 @@
     return (outputs, d_inputs) + tuple(summed)
 
 
+HEAD_LANES = 2 * HEAD_DIM
+
+
+def dot_nt(left, right):
+    return lax.dot_general(left, right, (((1,), (1,)), ((), ())), preferred_element_type=jnp.float32)
+
+
+def dot_nn(left, right):
+    return lax.dot_general(left, right, (((1,), (0,)), ((), ())), preferred_element_type=jnp.float32)
+
+
+def dot_tn(left, right):
+    return lax.dot_general(left, right, (((0,), (0,)), ((), ())), preferred_element_type=jnp.float32)
+
+
+def head_lane_masks(rows):
+    lane = lax.broadcasted_iota(jnp.int32, (rows, HEAD_LANES), 1)
+    limit = jnp.where(pl.program_id(0) == pl.num_programs(0) - 1, HEAD_DIM * (2 - HEADS % 2), HEAD_LANES)
+    return (lane < HEAD_DIM), (lane >= HEAD_DIM) & (lane < limit)
+
+
+def allowed_bias(low_ref, high_ref, rpos_ref, rseg_ref, cpos_ref, cseg_ref):
+    half = rpos_ref.shape[0] // 2
+    for ref, start, pieces in (
+        (low_ref, 0, ((0, half), (2 * half, 3 * half))),
+        (high_ref, half, ((0, half), (2 * half, 3 * half), (3 * half, 4 * half), (half, 2 * half))),
+    ):
+        rpos = rpos_ref[start : start + half, :]
+        rseg = rseg_ref[start : start + half, :]
+        at = 0
+        for first, last in pieces:
+            fits = (cpos_ref[:, first:last] <= rpos) & (cseg_ref[:, first:last] == rseg)
+            ref[:, at : at + half] = jnp.where(fits, 0.0, -1e30)
+            at += half
+
+
+def gather_keys(own, other, half):
+    low = jnp.concatenate([own[:half], other[:half]], 0)
+    high = jnp.concatenate([own[:half], other, own[half:]], 0)
+    return low, high
+
+
+def attend_kernel(rpos, rseg, cpos, cseg, q_ref, ko_ref, kp_ref, vo_ref, vp_ref, out_ref, lse_ref, low_ref, high_ref):
+    rows = q_ref.shape[0]
+    half = rows // 2
+
+    @pl.when(pl.program_id(0) == 0)
+    def _():
+        allowed_bias(low_ref, high_ref, rpos, rseg, cpos, cseg)
+
+    first, second = head_lane_masks(rows)
+    zero = jnp.zeros((), jnp.bfloat16)
+    queries = q_ref[...]
+    keys_own = jnp.where(first | second, ko_ref[...], zero)
+    keys_other = jnp.where(first | second, kp_ref[...], zero)
+    values_own, values_other = vo_ref[...], vp_ref[...]
+    outs = [None, None]
+    for head, lanes in enumerate((first, second)):
+        query = jnp.where(lanes, queries, zero)
+        v_own = jnp.where(lanes, values_own, zero)
+        v_other = jnp.where(lanes, values_other, zero)
+        key_parts = gather_keys(keys_own, keys_other, half)
+        value_parts = gather_keys(v_own, v_other, half)
+        for part, bias_ref in enumerate((low_ref, high_ref)):
+            scores = dot_nt(query[part * half : (part + 1) * half], key_parts[part]) + bias_ref[...]
+            top = jnp.max(scores, -1, keepdims=True)
+            expo = jnp.exp(scores - top)
+            total = jnp.sum(expo, -1, keepdims=True)
+            mixed = dot_nn(expo.astype(jnp.bfloat16), value_parts[part]) / total
+            outs[part] = mixed if outs[part] is None else outs[part] + mixed
+            lse_ref[part * half : (part + 1) * half, head : head + 1] = top + jnp.log(total)
+    out_ref[...] = jnp.concatenate(outs, 0).astype(jnp.bfloat16)
+
+
+def attend_back_kernel(
+    rpos, rseg, cpos, cseg, q_ref, ko_ref, kp_ref, vo_ref, vp_ref, do_ref, lse_ref,
+    dq_ref, dko_ref, dkp_ref, dvo_ref, dvp_ref, low_ref, high_ref,
+):
+    rows = q_ref.shape[0]
+    half = rows // 2
+
+    @pl.when(pl.program_id(0) == 0)
+    def _():
+        allowed_bias(low_ref, high_ref, rpos, rseg, cpos, cseg)
+
+    first, second = head_lane_masks(rows)
+    zero = jnp.zeros((), jnp.bfloat16)
+    queries, grads = q_ref[...], do_ref[...]
+    both = first | second
+    keys_own = jnp.where(both, ko_ref[...], zero)
+    keys_other = jnp.where(both, kp_ref[...], zero)
+    values_own = jnp.where(both, vo_ref[...], zero)
+    values_other = jnp.where(both, vp_ref[...], zero)
+    key_sums, value_sums = [None] * 4, [None] * 4
+    query_sums = [None, None]
+
+    def add(sums, at, new):
+        sums[at] = new if sums[at] is None else sums[at] + new
+
+    order = ((0, 2), (0, 2, 3, 1))
+    for head, lanes in enumerate((first, second)):
+        query = jnp.where(lanes, queries, zero)
+        grad = jnp.where(lanes, grads, zero)
+        key_own = jnp.where(lanes, keys_own, zero)
+        key_other = jnp.where(lanes, keys_other, zero)
+        key_parts = gather_keys(key_own, key_other, half)
+        value_parts = gather_keys(values_own, values_other, half)
+        for part, bias_ref in enumerate((low_ref, high_ref)):
+            span = slice(part * half, (part + 1) * half)
+            scores = dot_nt(query[span], key_parts[part]) + bias_ref[...]
+            probs = jnp.exp(scores - lse_ref[span, head : head + 1])
+            d_probs = dot_nt(grad[span], value_parts[part])
+            weighed = probs * d_probs
+            delta = jnp.sum(weighed, -1, keepdims=True)
+            d_scores = (weighed - probs * delta).astype(jnp.bfloat16)
+            add(query_sums, part, dot_nn(d_scores, key_parts[part]))
+            d_key = dot_tn(d_scores, query[span])
+            d_value = dot_tn(probs.astype(jnp.bfloat16), grad[span])
+            for at, block in enumerate(order[part]):
+                add(key_sums, block, d_key[at * half : (at + 1) * half])
+                add(value_sums, block, d_value[at * half : (at + 1) * half])
+    dq_ref[...] = jnp.concatenate(query_sums, 0) * HEAD_DIM ** (-0.5)
+    dko_ref[...] = jnp.concatenate(key_sums[:2], 0)
+    dkp_ref[...] = jnp.concatenate(key_sums[2:], 0).astype(jnp.bfloat16)
+    dvo_ref[...] = jnp.concatenate(value_sums[:2], 0)
+    dvp_ref[...] = jnp.concatenate(value_sums[2:], 0).astype(jnp.bfloat16)
+
+
+def attention_specs(rows, extra):
+    whole = lambda shape: pl.BlockSpec(shape, lambda j: (0, 0))
+    block = pl.BlockSpec((rows, HEAD_LANES), lambda j: (0, j))
+    ins = [whole((rows, 1)), whole((rows, 1)), whole((1, 2 * rows)), whole((1, 2 * rows))]
+    return ins, block
+
+
+def attend(marks, queries, own_k, other_k, own_v, other_v):
+    rows, features = queries.shape
+    pairs = pl.cdiv(features, HEAD_LANES)
+    ins, block = attention_specs(rows, 0)
+    lse = pl.BlockSpec((None, rows, 2), lambda j: (j, 0, 0))
+    return pl.pallas_call(
+        attend_kernel,
+        grid=(pairs,),
+        in_specs=ins + [block] * 5,
+        out_specs=[block, lse],
+        out_shape=[
+            jax.ShapeDtypeStruct((rows, features), jnp.bfloat16),
+            jax.ShapeDtypeStruct((pairs, rows, 2), jnp.float32),
+        ],
+        scratch_shapes=[pltpu.VMEM((rows // 2, rows), jnp.float32), pltpu.VMEM((rows // 2, 2 * rows), jnp.float32)],
+        cost_estimate=pl.CostEstimate(flops=8 * rows * rows * features, bytes_accessed=12 * rows * features, transcendentals=0),
+        name="attend",
+    )(*marks, queries, own_k, other_k, own_v, other_v)
+
+
+def attend_back(marks, queries, own_k, other_k, own_v, other_v, grads, lse_rows):
+    rows, features = queries.shape
+    pairs = pl.cdiv(features, HEAD_LANES)
+    ins, block = attention_specs(rows, 0)
+    lse = pl.BlockSpec((None, rows, 2), lambda j: (j, 0, 0))
+    wide = jax.ShapeDtypeStruct((rows, features), jnp.float32)
+    slim = jax.ShapeDtypeStruct((rows, features), jnp.bfloat16)
+    return pl.pallas_call(
+        attend_back_kernel,
+        grid=(pairs,),
+        in_specs=ins + [block] * 6 + [lse],
+        out_specs=[block] * 5,
+        out_shape=[wide, wide, slim, wide, slim],
+        scratch_shapes=[pltpu.VMEM((rows // 2, rows), jnp.float32), pltpu.VMEM((rows // 2, 2 * rows), jnp.float32)],
+        cost_estimate=pl.CostEstimate(flops=20 * rows * rows * features, bytes_accessed=30 * rows * features, transcendentals=0),
+        name="attend_back",
+    )(*marks, queries, own_k, other_k, own_v, other_v, grads, lse_rows)
+
+
+def trade_lists(shard_count, rep_count):
+    first, second = [], []
+    for shard in range(shard_count):
+        for rep in range(rep_count):
+            core = rep % 2
+            outer = (shard >= shard_count // 2) * 1
+            target_core = 0 if shard in (0, shard_count - 1) else 1
+            for moves, local in ((first, outer), (second, 1 - outer)):
+                target = (2 * core + local) * rep_count + (rep - core + target_core)
+                moves.append((shard * rep_count + rep, target))
+    return first, second
+
+
+BOTH = ("shard", "rep")
+
+
+def to_sequence(blocks, moves, shard_index):
+    upper = shard_index >= 2
+    one = lax.ppermute(jnp.where(upper, blocks[1], blocks[0]), BOTH, moves[0])
+    two = lax.ppermute(jnp.where(upper, blocks[0], blocks[1]), BOTH, moves[1])
+    even = shard_index % 2 == 0
+    return jnp.concatenate([jnp.where(even, one, two), jnp.where(even, two, one)], 0)
+
+
+def from_sequence(rows, moves, shard_index):
+    half = rows.shape[0] // 2
+    low, high = rows[:half], rows[half:]
+    even = shard_index % 2 == 0
+    back = [[(b, a) for a, b in move] for move in moves]
+    one = lax.ppermute(jnp.where(even, low, high), BOTH, back[0])
+    two = lax.ppermute(jnp.where(even, high, low), BOTH, back[1])
+    upper = shard_index >= 2
+    return jnp.stack([jnp.where(upper, two, one), jnp.where(upper, one, two)])
+
+
+def swap_core(array, rep_count):
+    return lax.ppermute(array, "rep", [(r, r ^ 1) for r in range(rep_count)])
+
+
+def gather_weights(w_qkv, w_out, w_fc1, w_fc2, smalls):
+    features = w_qkv.shape[0]
+    rep = lax.axis_index("rep")
+    part = w_out.shape[1]
+    side = jnp.concatenate([w_qkv, w_out, w_fc1], 1)
+    piece = lax.dynamic_slice(side, (0, rep * part), (features, part)).T
+    half = part // 2
+    tail = lax.dynamic_slice(w_fc2, ((rep // 2) * features, (rep % 2) * half), (features, half)).T
+    small = jnp.zeros((8, features), jnp.bfloat16).at[:3].set(smalls)
+    head = lax.all_gather(jnp.concatenate([piece, small], 0), BOTH, axis=0).reshape(4, 8, part + 8, features)
+    rest = lax.all_gather(tail, BOTH, axis=0).reshape(4, 4, part, features)
+    qkv = head[:, 0:3, :part].reshape(3 * features, features)
+    out = head[:, 3, :part].reshape(features, features)
+    fc1 = head[:, 4:8, :part].reshape(4 * features, features)
+    fc2 = rest.transpose(1, 0, 2, 3).reshape(4, features, features)
+    return qkv, out, fc1, fc2, head[:, 0, part : part + 3]
+
+
+def reduce_rows(grads):
+    rows = lax.psum_scatter(grads.astype(jnp.bfloat16), "rep", scatter_dimension=1, tiled=True)
+    rows = lax.psum_scatter(rows, "shard", scatter_dimension=0, tiled=True)
+    return lax.all_gather(rows, "rep", axis=1, tiled=True)[0]
+
+
+def shards_by_sequence(
+    inputs, segments, cotangent, ln_gain, ln_bias, w_qkv, qv_bias, w_out, out_bias, w_fc1, fc1_bias, w_fc2
+):
+    features = inputs.shape[2]
+    block = inputs.shape[1]
+    rep_count = lax.axis_size("rep")
+    moves = trade_lists(4, rep_count)
+    shard_index = lax.axis_index("shard")
+    core = lax.axis_index("rep") % 2
+    f32 = jnp.float32
+    smalls = jnp.concatenate(
+        [ln_gain.reshape(-1), ln_bias.reshape(-1), qv_bias.reshape(-1), out_bias.reshape(-1), fc1_bias.reshape(-1)]
+    ).reshape(3, features)
+    wq, wo, w1, w2, small_rows = gather_weights(w_qkv, w_out, w_fc1, w_fc2, smalls)
+    small_rows = small_rows.reshape(4, 3 * features).astype(f32)
+    part = features // 4
+    gains = [small_rows[:, 0:part].reshape(-1), small_rows[:, part : 2 * part].reshape(-1)]
+    biases = [small_rows[:, 2 * part : 3 * part].reshape(-1), small_rows[:, 3 * part : 4 * part].reshape(-1)]
+    qv_row = small_rows[:, 4 * part : 6 * part].reshape(-1)
+    out_rows = [small_rows[:, 6 * part : 7 * part].reshape(-1), small_rows[:, 7 * part : 8 * part].reshape(-1)]
+    fc1_row = small_rows[:, 8 * part :].reshape(-1)
+
+    tokens = to_sequence(inputs, moves, shard_index).astype(f32)
+    d_output = to_sequence(cotangent, moves, shard_index)
+    partner_segments = swap_core(segments, rep_count)
+    mine_has = (shard_index // 2) == core
+    local = shard_index % 2
+    seg_row = jnp.where(
+        mine_has,
+        lax.dynamic_index_in_dim(segments, local, 0, keepdims=False),
+        lax.dynamic_index_in_dim(partner_segments, local, 0, keepdims=False),
+    )
+    low_own = jnp.where(core == 0, 0, 1)
+    high_own = jnp.where(core == 0, 3, 2)
+    spots = jnp.stack([low_own, high_own, 1 - low_own, 5 - high_own])
+    pos = (spots[:, None] * block + jnp.arange(block, dtype=jnp.int32)[None]).reshape(-1)
+    segs = seg_row.reshape(4, block)
+    seg = jnp.concatenate([lax.dynamic_index_in_dim(segs, spots[i], 0, keepdims=False) for i in range(4)])
+    rows = 2 * block
+    marks = (pos[:rows, None], seg[:rows, None], pos[None], seg[None])
+
+    normed_f32, unit_one, factor_one = layer_norm(tokens, gains[0], biases[0])
+    normed_one = normed_f32.astype(jnp.bfloat16)
+    own_k = dot_nt(normed_one, wq[features : 2 * features]).astype(jnp.bfloat16)
+    own_v = (dot_nt(normed_one, wq[2 * features :]) + qv_row[features:]).astype(jnp.bfloat16)
+    other_k, other_v = swap_core(own_k, rep_count), swap_core(own_v, rep_count)
+    queries = (dot_nt(normed_one, wq[:features]) + qv_row[:features]).astype(jnp.bfloat16)
+    queries = queries * jnp.asarray(HEAD_DIM ** (-0.5), jnp.bfloat16)
+    attn_mixed, lse_rows = attend(marks, queries, own_k, other_k, own_v, other_v)
+    residual = tokens + (dot_nt(attn_mixed, wo) + out_rows[0])
+    normed_f32, unit_two, factor_two = layer_norm(residual, gains[1], biases[1])
+    normed_two = normed_f32.astype(jnp.bfloat16)
+    pre_act = dot_nt(normed_two, w1) + fc1_row
+    activated_f32, gelu_pull = jax.vjp(gelu_tanh, pre_act)
+    activated = activated_f32.astype(jnp.bfloat16)
+    output = residual + out_rows[1]
+    for i in range(4):
+        output = output + dot_nt(activated[:, i * features : (i + 1) * features], w2[i])
+    outputs = from_sequence(output.astype(jnp.bfloat16), moves, shard_index)
+
+    d_out_f32 = d_output.astype(f32)
+    d_act = jnp.concatenate([dot_nn(d_output, w2[i]) for i in range(4)], 1)
+    d_pre = gelu_pull(d_act)[0].astype(jnp.bfloat16)
+    g_fc1 = dot_tn(d_pre, normed_two).reshape(4, features, features)
+    g_fc2 = jnp.stack(
+        [dot_tn(d_output, activated[:, i * features : (i + 1) * features]).reshape(4, part, features) for i in range(4)], 1
+    ).reshape(4, features, features)
+    fc_owned = reduce_rows(jnp.concatenate([g_fc1, g_fc2], 1))
+    g_fc1_row = jnp.sum(d_pre.astype(f32), 0)
+    d_norm_two = dot_nn(d_pre, w1)
+    d_residual = d_out_f32 + norm_back(d_norm_two, unit_two, factor_two, gains[1])
+    g_gain_two = jnp.sum(d_norm_two * unit_two, 0)
+    g_bias_two = jnp.sum(d_norm_two, 0)
+    d_branch = d_residual.astype(jnp.bfloat16)
+    d_mixed = dot_nn(d_branch, wo).astype(jnp.bfloat16)
+    d_q, dk_own, dk_other, dv_own, dv_other = attend_back(
+        marks, queries, own_k, other_k, own_v, other_v, d_mixed, lse_rows
+    )
+    d_q = d_q.astype(jnp.bfloat16)
+    d_k = (dk_own + swap_core(dk_other, rep_count).astype(f32)).astype(jnp.bfloat16)
+    d_v = (dv_own + swap_core(dv_other, rep_count).astype(f32)).astype(jnp.bfloat16)
+    g_wout = dot_tn(d_branch, attn_mixed).reshape(4, part, features)
+    g_wqkv = jnp.concatenate([dot_tn(d, normed_one) for d in (d_q, d_k, d_v)], 0).reshape(4, 3 * part, features)
+    d_norm_one = (
+        dot_nn(d_q, wq[:features]) + dot_nn(d_k, wq[features : 2 * features]) + dot_nn(d_v, wq[2 * features :])
+    )
+    d_tokens = d_residual + norm_back(d_norm_one, unit_one, factor_one, gains[0])
+    d_inputs = from_sequence(d_tokens.astype(jnp.bfloat16), moves, shard_index)
+    g_qv_row = jnp.concatenate([jnp.sum(d_q.astype(f32), 0), jnp.sum(d_v.astype(f32), 0)])
+    side_grads = [
+        jnp.sum(d_norm_one * unit_one, 0),
+        g_gain_two,
+        jnp.sum(d_norm_one, 0),
+        g_bias_two,
+        g_qv_row,
+        jnp.sum(d_branch.astype(f32), 0),
+        jnp.sum(d_out_f32, 0),
+        g_fc1_row,
+    ]
+    small_grads = jnp.concatenate([item.reshape(4, -1) for item in side_grads], 1)
+    small_owned = lax.psum(lax.psum_scatter(small_grads, "shard", scatter_dimension=0, tiled=True), "rep")[0]
+    attn_owned = reduce_rows(jnp.concatenate([g_wqkv, g_wout], 1))
+
+    def back(rows_in):
+        return rows_in.T.astype(f32)
+
+    g_fc2_owned = fc_owned[features:].reshape(4, part, features).transpose(0, 2, 1).reshape(4 * features, part)
+    return (
+        outputs,
+        d_inputs,
+        small_owned[: 2 * part].reshape(2, part),
+        small_owned[2 * part : 4 * part].reshape(2, part),
+        back(attn_owned[: 3 * part]),
+        small_owned[4 * part : 6 * part].reshape(1, 2 * part),
+        back(attn_owned[3 * part :]),
+        small_owned[6 * part : 8 * part].reshape(2, part),
+        back(fc_owned[:features]),
+        small_owned[8 * part :].reshape(1, 4 * part),
+        g_fc2_owned.astype(f32),
+    )
+
+
 def solution(mesh):
+    shard_count, rep_count = mesh.shape["shard"], mesh.shape["rep"]
+    by_sequence = shard_count == 4 and rep_count == 8
     placed = (
         P("rep", "shard", None),
         P("rep", None),
@@ -392,7 +755,7 @@
         P(None, "shard"),
     )
     return jax.shard_map(
-        shards,
+        shards_by_sequence if by_sequence else shards,
         mesh=mesh,
         in_specs=placed,
         out_specs=(

time: 2240 us -> 965 us (0.43)
  waiting for transfers between devices: 1500 us -> 431 us
  matrix products: 279 us -> 128 us
  local copies, waits for them, and re-layouts: 248 us -> 184 us
  Pallas kernels: 0 us -> 51.6 us
  loops' own time: 29.5 us -> 0 us
  starting transfers between devices: 0.98 us -> 29 us
  blocking collectives: 81.7 us -> 56.8 us
    all_gather x12 -> x4, waiting for transfers between devices: 733 us -> 150 us  [the longest x1 122 us: gather_weights(): lax.all_gather(jnp.concatenate([piece, small], 0), BOTH, axis=0)]
    unnamed x21 -> x10, waiting for transfers between devices: 367 us -> 63 us
    dot_general x60 -> x27, matrix products: 279 us -> 128 us  [the longest x9 47.3 us: dot_nt(): lax.dot_general(left, right, (((1,), (1,)), ((), ())), preferred_element_...]
    reduce_scatter x4 -> x2, waiting for transfers between devices: 310 us -> 170 us  [the longest x1 129 us: reduce_rows(): lax.psum_scatter(grads.astype(jnp.bfloat16), 'rep', scatter_dimension=1,...]
    psum x1 -> x0, waiting for transfers between devices: 91 us -> none  [shards(): lax.psum(owned[2].astype(jnp.bfloat16), 'rep').astype(jnp.float32)]
    while x245 -> x0, local copies, waits for them, and re-layouts: 55.4 us -> none
    pallas_call x0 -> x2, Pallas kernels: none -> 51.6 us  [the longest x1 32.7 us: attend_back(): pl.pallas_call(attend_back_kernel, grid=(pairs,), in_specs=ins + [block]...]
    ppermute x0 -> x13, waiting for transfers between devices: none -> 48.2 us  [the longest x2 48.1 us: to_sequence(): two = lax.ppermute(jnp.where(upper, blocks[0], blocks[1]), BOTH, moves[1])]
  transfers between devices with their start and end apart: 24 -> 21, of which waited for: 23 -> 8; matrix products, arithmetic and copies ran while one was open for 11% -> 21% of each run, Pallas kernels for 0% -> 0%
where the time goes in v1:
time: 965 us; the launch traced here: 959 us
  waiting for transfers between devices  431 us (45%)
  local copies, waits for them, and re-layouts  184 us (19%)
  matrix products  128 us (13%)
  other arithmetic  63 us (7%)
  blocking collectives  56.8 us (6%)
  Pallas kernels  51.6 us (5%)
  starting transfers between devices  29 us (3%)
  between operations  15.1 us (2%)
    reduce_scatter x1, waiting for transfers between devices, reduce_rows(): lax.psum_scatter(grads.astype(jnp.bfloat16), 'rep', scatter_dimension=1,...  129 us
    all_gather x1, waiting for transfers between devices, gather_weights(): lax.all_gather(jnp.concatenate([piece, small], 0), BOTH, axis=0)  122 us
    unnamed x84, local copies, waits for them, and re-layouts  72 us
    unnamed x10, waiting for transfers between devices  63 us
    ppermute x2, waiting for transfers between devices, to_sequence(): two = lax.ppermute(jnp.where(upper, blocks[0], blocks[1]), BOTH, moves[1])  48.1 us
    dot_general x9, matrix products, dot_nt(): lax.dot_general(left, right, (((1,), (1,)), ((), ())), preferred_element_...  47.3 us
    dot_general x9, matrix products, dot_nn(): lax.dot_general(left, right, (((1,), (0,)), ((), ())), preferred_element_...  43.7 us
    reduce_scatter x1, waiting for transfers between devices, reduce_rows(): rows = lax.psum_scatter(rows, 'shard', scatter_dimension=0, tiled=True)  41.3 us
  transfers between devices with their start and end apart: 21, of which 8 were waited for; matrix products, arithmetic and copies ran while one was open for 21% of the time, Pallas kernels for 0%

profile of v1, /device:TPU:0, one launch (start us, length us, event | category | flops | bytes accessed | tf_op | source)
XLA Modules:
  0.0 958.6 jit_solution(5618994978580122725)
XLA Ops:
  42.0 29.0 %collective-permute-done.1 = bf16[256,1088]{0,1:T(8,128)(2,1)} collective-permute-done((bf16[256,1088]{0,1:T(8,128)(2,1)S(1)}, bf16[256,1088]{0,1:T(8,128)(2,1)}, u32[]{:S(2)}, u32[]{:S(2)}) %collective-permute-start.1) | collective-permute-done | bytes 557088 | tf_op jit(solution)/shard_map/ppermute | solution.py:574
  72.9 19.2 %collective-permute-done.8 = bf16[256,1088]{0,1:T(8,128)(2,1)S(1)} collective-permute-done((bf16[256,1088]{0,1:T(8,128)(2,1)S(1)}, bf16[256,1088]{0,1:T(8,128)(2,1)S(1)}, u32[]{:S(2)}, u32[]{:S(2)}) %collective-permute-start.8) | collective-permute-done | bytes 557088 | tf_op jit(solution)/shard_map/ppermute | solution.py:574
  92.1 28.4 %all-gather.13.cloned.1.call-done = bf16[4352,1088]{1,0:T(8,128)(2,1)} async-done(((bf16[136,1088]{1,0:T(8,128)(2,1)}), bf16[4352,1088]{1,0:T(8,128)(2,1)}) %all-gather.13.cloned.1.call-update) | async-done | bytes 9469968 | tf_op jit(solution)/shard_map/all_gather | solution.py:604
  133.2 121.5 %all-gather.11.cloned.1.call-done = bf16[8960,1088]{1,0:T(8,128)(2,1)} async-done(((bf16[280,1088]{1,0:T(8,128)(2,1)}), bf16[8960,1088]{1,0:T(8,128)(2,1)}) %all-gather.11.cloned.1.call-update) | async-done | bytes 19496976 | tf_op jit(solution)/shard_map/all_gather | solution.py:603
  283.0 11.5 %concatenate.60 = f32[512,4352]{1,0:T(8,128)} concatenate(f32[512,1088]{1,0:T(8,128)} %fusion.57, f32[512,1088]{1,0:T(8,128)} %fusion.56, f32[512,1088]{1,0:T(8,128)} %fusion.55, f32[512,1088]{1,0:T(8,128)} %fusion.54), dimensions={1} | concatenate | bytes 17825792 | tf_op jit(solution)/shard_map/concatenate | solution.py:679
  297.9 8.4 slice.235
  318.9 18.9 %attend.1 = (bf16[512,1088]{1,0:T(8,128)(2,1)}, f32[9,512,2]{2,1,0:T(8,128)}) custom-call(s32[512,1]{1,0:T(8,128)} %bitcast.156, s32[512,1]{1,0:T(8,128)} %copy.115.rseg, s32[1,1024]{1,0:T(1,128)} %bitcast.164, s32[1,1024]{1,0:T(1,128)} %bitcast.166, bf16[512,1088]{1,0:T(8,128)(2,1)} %fusion.11.q_ref, bf16[512,1088]{1,0:T(8,128)(2,1)} %copy.116.ko_ref, ...), custom_call_target="tpu_custom_call" | custom-call | flops 2281701376 | bytes 6684672 | tf_op jit(solution)/shard_map/attend/pallas_call | solution.py:521
  343.3 13.5 %fusion.53 = f32[512,4352]{1,0:T(8,128)} fusion(bf16[4352,1088]{1,0:T(8,128)(2,1)} %bitcast.129, f32[512,1088]{0,1:T(8,128)} %copy-done.8, f32[1088]{0:T(1024)S(1)} %add.232, f32[1088]{0:T(1024)S(1)} %mul.174, f32[512]{0:T(512)S(1)} %add_rsqrt_fusion, f32[512]{0:T(512)S(1)} %broadcast_multiply_fusion.4), kind=kOutput, calls=%fused_computation.153 | convolution fusion | flops 4851400704 | bytes 20623872 | tf_op jit(solution)/shard_map/dot_general | solution.py:385
  356.8 11.7 %convert_reduce_fusion = (f32[4352]{0:T(1024)S(1)}, bf16[512,4352]{1,0:T(8,128)(2,1)}, bf16[512,4352]{1,0:T(8,128)(2,1)}) fusion(f32[512,4352]{1,0:T(8,128)S(1)} %bitcast.122, f32[512,4352]{1,0:T(8,128)} %fusion.53, f32[4352]{0:T(1024)S(1)} %add.235), kind=kLoop, calls=%fused_computation.14 | loop fusion | flops 55701248 | bytes 26773504 | tf_op jit(solution)/shard_map/reduce_sum | solution.py:686
  368.5 13.8 %multiply_reduce_fusion = (f32[1088]{0:T(1024)S(1)}, f32[512]{0:T(512)S(1)}, f32[512]{0:T(512)S(1)}, f32[1088]{0:T(1024)S(1)}, f32[512,1088]{0,1:T(8,128)S(1)}) fusion(f32[512,1088]{0,1:T(8,128)} %copy-done.8, f32[512]{0:T(512)S(1)} %add_rsqrt_fusion, f32[512]{0:T(512)S(1)} %broadcast_multiply_fusion.4, f32[1088]{0:T(1024)S(1)} %mul.174, ...), kind=kOutput, calls=%fused_computation.71 | convolution fusion | flops 4853625856 | bytes 18404096 | tf_op jit(solution)/shard_map/dot_general | solution.py:389
  388.0 32.7 %attend_back.1 = (f32[512,1088]{1,0:T(8,128)}, f32[512,1088]{1,0:T(8,128)}, bf16[512,1088]{1,0:T(8,128)(2,1)}, f32[512,1088]{1,0:T(8,128)}, bf16[512,1088]{1,0:T(8,128)(2,1)}) custom-call(s32[512,1]{1,0:T(8,128)} %bitcast.157, s32[512,1]{1,0:T(8,128)} %copy.115.rseg, s32[1,1024]{1,0:T(1,128)} %bitcast.165, s32[1,1024]{1,0:T(1,128)} %bitcast.167, ...), custom_call_target="tpu_custom_call" | custom-call | flops 5704253440 | bytes 16711680 | tf_op jit(solution)/shard_map/attend_back/pallas_call | solution.py:543
  447.2 12.5 %concatenate.65 = bf16[3264,1088]{0,1:T(8,128)(2,1)} concatenate(bf16[1088,1088]{0,1:T(8,128)(2,1)} %convolution_convert_fusion.3, bf16[1088,1088]{0,1:T(8,128)(2,1)} %convolution_convert_fusion.2, bf16[1088,1088]{0,1:T(8,128)(2,1)} %convolution_convert_fusion.1), dimensions={0} | concatenate | bytes 14204928 | tf_op jit(solution)/shard_map/concatenate | solution.py:700
  459.6 11.1 %copy.133 = bf16[3264,1088]{1,0:T(8,128)(2,1)} copy(bf16[3264,1088]{0,1:T(8,128)(2,1)} %concatenate.65) | data formatting | bytes 14204928 | tf_op jit(solution)/shard_map/concatenate | solution.py:700
  476.9 26.9 %copy.154 = bf16[4,1088,1088]{2,0,1:T(4,128)(2,1)} copy(bf16[4,1088,1088]{2,1,0:T(8,128)(2,1)S(1)} %pad_maximum_fusion.1) | data formatting | bytes 18939904
  503.7 16.6 %reshape.327 = bf16[1088,4352]{1,0:T(8,128)(2,1)} reshape(bf16[1088,4,1088]{2,1,0:T(4,128)(2,1)} %bitcast.120) | data formatting | bytes 18939904
  520.4 10.4 %convolution_convert_fusion = bf16[4352,1088]{0,1:T(8,128)(2,1)} fusion(bf16[512,4352]{1,0:T(8,128)(2,1)} %get-tuple-element.93, f32[512,1088]{0,1:T(8,128)} %copy-done.8, f32[1088]{0:T(1024)S(1)} %add.232, f32[1088]{0:T(1024)S(1)} %mul.174, f32[512]{0:T(512)S(1)} %add_rsqrt_fusion, f32[512]{0:T(512)S(1)} %broadcast_multiply_fusion.4), kind=kOutput, calls=%fused_computation.1 | convolution fusion | flops 4856135680 | bytes 16167424 | tf_op jit(solution)/shard_map/dot_general | solution.py:393
  530.8 14.0 %copy.147 = bf16[4352,1088]{1,0:T(8,128)(2,1)} copy(bf16[4352,1088]{0,1:T(8,128)(2,1)} %convolution_convert_fusion) | data formatting | bytes 18939904 | tf_op jit(solution)/shard_map/reshape | solution.py:681
  558.8 9.7 %pad_maximum_fusion = bf16[4,2176,1088]{2,1,0:T(8,128)(2,1)} fusion(bf16[4,1088,1088]{2,1,0:T(8,128)(2,1)S(1)} %bitcast.119, bf16[4,1088,1088]{2,1,0:T(8,128)(2,1)S(1)} %bitcast.118), kind=kLoop, calls=%fused_computation | loop fusion | flops 37879808 | bytes 37879808 | tf_op jit(solution)/shard_map/concatenate | solution.py:685
  568.6 29.9 %reduce-scatter.13.cloned.1.call-done = bf16[136,4352]{1,0:T(8,128)(2,1)} async-done(((bf16[1088,4352]{1,0:T(8,128)(2,1)}), bf16[136,4352]{1,0:T(8,128)(2,1)}) %reduce-scatter.13.cloned.1.call-update) | async-done | bytes 1183760
  604.9 129.0 %reduce-scatter.9.cloned.1.call-done = bf16[4,272,1088]{2,1,0:T(8,128)(2,1)} async-done(((bf16[4,2176,1088]{2,1,0:T(8,128)(2,1)}), bf16[4,272,1088]{2,1,0:T(8,128)(2,1)}) %reduce-scatter.9.cloned.1.call-update) | async-done | bytes 2367504 | tf_op jit(solution)/shard_map/reduce_scatter | solution.py:613
  734.0 32.9 %reduce-scatter.15.cloned.1.call-done = bf16[1,136,1088]{2,1,0:T(8,128)(2,1)} async-done(((bf16[4,136,1088]{2,1,0:T(8,128)(2,1)}), bf16[1,136,1088]{2,1,0:T(8,128)(2,1)}) %reduce-scatter.15.cloned.1.call-update) | async-done | bytes 295952
  777.3 41.3 %reduce-scatter.11.cloned.1.call-done = bf16[1,272,1088]{2,1,0:T(8,128)(2,1)} async-done(((bf16[4,272,1088]{2,1,0:T(8,128)(2,1)}), bf16[1,272,1088]{2,1,0:T(8,128)(2,1)}) %reduce-scatter.11.cloned.1.call-update) | async-done | bytes 591888 | tf_op jit(solution)/shard_map/reduce_scatter | solution.py:614
  858.3 34.1 %all-reduce.1 = f32[4,3264]{1,0:T(4,128)S(1)} all-reduce(f32[4,3264]{1,0:T(4,128)S(1)} %concatenate.64), channel_id=4, replica_groups=mesh['shard'=4,'rep'=8] {'shard'}, use_global_device_ids=true, to_apply=%region_17.18.clone | all-reduce | flops 13056 | bytes 104448
  893.1 22.6 %psum.7 = f32[1,3264]{1,0:T(1,128)S(1)} all-reduce(f32[1,3264]{1,0:T(1,128)S(1)} %constant_dynamic-slice_fusion.4), channel_id=1, replica_groups=mesh['shard'=4,'rep'=8] {'rep'}, use_global_device_ids=true, to_apply=%region_18.19 | all-reduce | flops 3264 | bytes 26112 | tf_op jit(solution)/shard_map/psum | solution.py:718
  (244 shorter events, 243.9 us)
Async XLA Ops:
  7.2 113.3 %all-gather.13.cloned.1.call-start = ((), (), s32[]{:S(2)}) async-start(), calls=%async_computation.9 | async-start | bytes 10340352 | tf_op jit(solution)/shard_map/all_gather | solution.py:604
  9.8 245.0 %all-gather.11.cloned.1.call-start = ((), (), s32[]{:S(2)}) async-start(), calls=%async_computation.8 | async-start | bytes 21288960 | tf_op jit(solution)/shard_map/all_gather | solution.py:603
  21.6 576.9 %reduce-scatter.13.cloned.1.call-start = ((), (), s32[]{:S(2)}) async-start(), calls=%async_computation.10 | async-start | bytes 10653696
  21.7 18.0 %collective-permute-start.2 = (s32[2,1024]{1,0:T(2,128)S(1)}, s32[2,1024]{1,0:T(2,128)S(1)}, u32[]{:S(2)}, u32[]{:S(2)}) collective-permute-start(s32[2,1024]{1,0:T(2,128)S(1)} %copy-done.26), channel_id=1, source_target_pairs={{0,1},{1,0},{2,3},{3,2},{4,5},{5,4},{6,7},{7,6},{8,9},{9,8},{10,11... | collective-permute-start | bytes 24584 | tf_op jit(solution)/shard_map/ppermute | solution.py:591
  23.1 18.1 %collective-permute-start = (bf16[256,1088]{0,1:T(8,128)(2,1)}, bf16[256,1088]{0,1:T(8,128)(2,1)S(1)}, u32[]{:S(2)}, u32[]{:S(2)}) collective-permute-start(bf16[256,1088]{0,1:T(8,128)(2,1)} %get-tuple-element.120), channel_id=1, source_target_pairs={{0,0},{1,16},{2,2},{3,18},{4,4},{5,20},{6,6},{7,22},{8,1},{9,17},{... | collective-permute-start | bytes 1671176 | tf_op jit(solution)/shard_map/ppermute | solution.py:573
  24.8 46.1 %collective-permute-start.1 = (bf16[256,1088]{0,1:T(8,128)(2,1)S(1)}, bf16[256,1088]{0,1:T(8,128)(2,1)}, u32[]{:S(2)}, u32[]{:S(2)}) collective-permute-start(bf16[256,1088]{0,1:T(8,128)(2,1)S(1)} %get-tuple-element.121), channel_id=1, source_target_pairs={{0,8},{1,24},{2,10},{3,26},{4,12},{5,28},{6,14},{7,30},{8,9},{9,25... | collective-permute-start | bytes 1671176 | tf_op jit(solution)/shard_map/ppermute | solution.py:574
  30.1 42.8 %collective-permute-start.7 = (bf16[256,1088]{0,1:T(8,128)(2,1)S(1)}, bf16[256,1088]{0,1:T(8,128)(2,1)S(1)}, u32[]{:S(2)}, u32[]{:S(2)}) collective-permute-start(bf16[256,1088]{0,1:T(8,128)(2,1)S(1)} %get-tuple-element.112), channel_id=1, source_target_pairs={{0,0},{1,16},{2,2},{3,18},{4,4},{5,20},{6,6},{7,22},{8,1},{9,17},{... | collective-permute-start | bytes 1671176 | tf_op jit(solution)/shard_map/ppermute | solution.py:573
  30.8 61.2 %collective-permute-start.8 = (bf16[256,1088]{0,1:T(8,128)(2,1)S(1)}, bf16[256,1088]{0,1:T(8,128)(2,1)S(1)}, u32[]{:S(2)}, u32[]{:S(2)}) collective-permute-start(bf16[256,1088]{0,1:T(8,128)(2,1)S(1)} %get-tuple-element.113), channel_id=1, source_target_pairs={{0,8},{1,24},{2,10},{3,26},{4,12},{5,28},{6,14},{7,30},{8,9},{9,25... | collective-permute-start | bytes 1671176 | tf_op jit(solution)/shard_map/ppermute | solution.py:574
  255.8 38.8 %copy-start.21 = (f32[4,3264]{1,0:T(4,128)}, f32[4,3264]{1,0:T(4,128)S(1)}, u32[]{:S(2)}) copy-start(f32[4,3264]{1,0:T(4,128)S(1)} %reshape.317) | copy-start | bytes 156676
  268.6 45.6 %collective-permute-start.3 = (bf16[512,1088]{0,1:T(8,128)(2,1)}, bf16[512,1088]{0,1:T(8,128)(2,1)}, u32[]{:S(2)}, u32[]{:S(2)}) collective-permute-start(bf16[512,1088]{0,1:T(8,128)(2,1)} %convolution_convert_fusion.9), channel_id=1, source_target_pairs={{0,1},{1,0},{2,3},{3,2},{4,5},{5,4},{6,7},{7,6},{8,9},{9,8},{10,11... | collective-permute-start | bytes 3342344 | tf_op jit(solution)/shard_map/ppermute | solution.py:591
  274.3 42.3 %collective-permute-start.4 = (bf16[512,1088]{0,1:T(8,128)(2,1)}, bf16[512,1088]{0,1:T(8,128)(2,1)}, u32[]{:S(2)}, u32[]{:S(2)}) collective-permute-start(bf16[512,1088]{0,1:T(8,128)(2,1)} %copy.113), channel_id=1, source_target_pairs={{0,1},{1,0},{2,3},{3,2},{4,5},{5,4},{6,7},{7,6},{8,9},{9,8},{10,11... | collective-permute-start | bytes 3342344 | tf_op jit(solution)/shard_map/ppermute | solution.py:591
  423.1 10.3 %collective-permute-start.10 = (bf16[512,1088]{0,1:T(8,128)(2,1)}, bf16[512,1088]{0,1:T(8,128)(2,1)}, u32[]{:S(2)}, u32[]{:S(2)}) collective-permute-start(bf16[512,1088]{0,1:T(8,128)(2,1)} %copy.131), channel_id=1, source_target_pairs={{0,1},{1,0},{2,3},{3,2},{4,5},{5,4},{6,7},{7,6},{8,9},{9,8},{10,11... | collective-permute-start | bytes 3342344 | tf_op jit(solution)/shard_map/ppermute | solution.py:591
  424.8 15.7 %collective-permute-start.9 = (bf16[512,1088]{0,1:T(8,128)(2,1)}, bf16[512,1088]{0,1:T(8,128)(2,1)}, u32[]{:S(2)}, u32[]{:S(2)}) collective-permute-start(bf16[512,1088]{0,1:T(8,128)(2,1)} %copy.129), channel_id=1, source_target_pairs={{0,1},{1,0},{2,3},{3,2},{4,5},{5,4},{6,7},{7,6},{8,9},{9,8},{10,11... | collective-permute-start | bytes 3342344 | tf_op jit(solution)/shard_map/ppermute | solution.py:591
  520.4 213.5 %reduce-scatter.9.cloned.1.call-start = ((), (), s32[]{:S(2)}) async-start(), calls=%async_computation.5 | async-start | bytes 22560768 | tf_op jit(solution)/shard_map/reduce_scatter | solution.py:613
  568.5 198.3 %reduce-scatter.15.cloned.1.call-start = ((), (), s32[]{:S(2)}) async-start(), calls=%async_computation.11 | async-start | bytes 1566720
  604.8 162.3 %copy-start.27 = (u32[32]{0:T(128)S(1)}, u32[32]{0:T(128)}, u32[]{:S(2)}) copy-start(u32[32]{0:T(128)} %constant.155) | copy-start | bytes 388
  604.8 162.9 %copy-start.22 = (f32[4,272]{1,0:T(4,128)S(1)}, f32[4,272]{1,0:T(4,128)}, u32[]{:S(2)}) copy-start(f32[4,272]{1,0:T(4,128)} %get-tuple-element.124) | copy-start | bytes 13060
  604.8 213.8 %reduce-scatter.11.cloned.1.call-start = ((), (), s32[]{:S(2)}) async-start(), calls=%async_computation.6 | async-start | bytes 3133440 | tf_op jit(solution)/shard_map/reduce_scatter | solution.py:614
  733.9 188.7 %all-gather.7.cloned.1.call-start = ((), (), s32[]{:S(2)}) async-start(), calls=%async_computation.4 | async-start | bytes 2820096 | tf_op jit(solution)/shard_map/all_gather | solution.py:615
  766.9 161.5 %all-gather.9.cloned.1.call-start = ((), (), s32[]{:S(2)}) async-start(), calls=%async_computation.7 | async-start | bytes 5640192 | tf_op jit(solution)/shard_map/all_gather | solution.py:615
  829.2 89.8 %collective-permute-start.5 = (bf16[256,1088]{0,1:T(8,128)(2,1)}, bf16[256,1088]{0,1:T(8,128)(2,1)}, u32[]{:S(2)}, u32[]{:S(2)}) collective-permute-start(bf16[256,1088]{0,1:T(8,128)(2,1)} %get-tuple-element.116), channel_id=1, source_target_pairs={{8,0},{24,1},{10,2},{26,3},{12,4},{28,5},{14,6},{30,7},{9,8},{25,9... | collective-permute-start | bytes 1671176 | tf_op jit(solution)/shard_map/ppermute | solution.py:585
  832.7 86.3 %collective-permute-start.6 = (bf16[256,1088]{0,1:T(8,128)(2,1)}, bf16[256,1088]{0,1:T(8,128)(2,1)}, u32[]{:S(2)}, u32[]{:S(2)}) collective-permute-start(bf16[256,1088]{0,1:T(8,128)(2,1)} %get-tuple-element.117), channel_id=1, source_target_pairs={{0,0},{16,1},{2,2},{18,3},{4,4},{20,5},{6,6},{22,7},{1,8},{17,9},{... | collective-permute-start | bytes 1671176 | tf_op jit(solution)/shard_map/ppermute | solution.py:584
  855.3 63.7 %collective-permute-start.11 = (bf16[256,1088]{0,1:T(8,128)(2,1)S(1)}, bf16[256,1088]{0,1:T(8,128)(2,1)S(1)}, u32[]{:S(2)}, u32[]{:S(2)}) collective-permute-start(bf16[256,1088]{0,1:T(8,128)(2,1)S(1)} %get-tuple-element.108), channel_id=1, source_target_pairs={{8,0},{24,1},{10,2},{26,3},{12,4},{28,5},{14,6},{30,7},{9,8},{25,9... | collective-permute-start | bytes 1671176 | tf_op jit(solution)/shard_map/ppermute | solution.py:585
  857.2 61.7 %collective-permute-start.12 = (bf16[256,1088]{0,1:T(8,128)(2,1)S(1)}, bf16[256,1088]{0,1:T(8,128)(2,1)S(1)}, u32[]{:S(2)}, u32[]{:S(2)}) collective-permute-start(bf16[256,1088]{0,1:T(8,128)(2,1)S(1)} %get-tuple-element.109), channel_id=1, source_target_pairs={{0,0},{16,1},{2,2},{18,3},{4,4},{20,5},{6,6},{22,7},{1,8},{17,9},{... | collective-permute-start | bytes 1671176 | tf_op jit(solution)/shard_map/ppermute | solution.py:584
  (34 other events, 169.7 us)
Sparse Core Ops, SparseCore 0:
  11.5 108.9 all-gather.12
  124.0 130.7 all-gather.10
  520.5 77.9 reduce-scatter.12
  602.1 131.7 reduce-scatter.8
  736.6 30.2 reduce-scatter.14
  769.1 49.5 reduce-scatter.10
  820.5 28.9 all-gather.6
  851.4 40.0 all-gather.8
